TPU v7x, 32 devices: a whole 2x2x4 slice. The times are simulated.
32 devices in a mesh: gx: 8 (over z, x), gy: 4 (over y, core).
Axes of the slice: x: 2, y: 2, z: 4, core: 2. Of those that a mesh axis runs over, the one named last changes fastest.
Arguments:
- mode_fields: float32 [32, 512, 1024], P(None, 'gx', 'gy'), may hold values from -60 to 60, as said below
- conductance: float32 [512, 1024], P('gx', 'gy'), may hold values from 0.5 to 2
- potential: float32 [512, 1024], P('gx', 'gy'), may hold values from 0.25 to 4
Outputs:
- basis_field: float32 [128, 512, 1024], P(None, 'gx', 'gy')
- scaled_factor: float32 [128, 128], replicated
Inputs may be any that keep to these rules, and one draw needn't show every extreme that they name: `mode_fields`: Real-valued mode amplitudes.
All inputs are finite; a program needn't handle non-finite values.
Results may differ from a plain program's by a relative error of at most 0.0003.
Values sent between devices are 32-bit elements; how exact they have to be, the bound alone decides.
A program may use at most 64 MiB of HBM per device.

v0:
```python
import jax
import jax.numpy as jnp
from jax import lax
from jax.sharding import PartitionSpec as P


def padded_2(value, sides, width):
    for axis, dim in sides:
        peers, length = (lax.axis_size(axis), value.shape[dim])
        up = [(i, (i + 1) % peers) for i in range(peers - 1)]
        down = [(j, i) for i, j in up]
        last = lax.slice_in_dim(value, length - width, length, axis=dim)
        first = lax.slice_in_dim(value, 0, width, axis=dim)
        before = lax.ppermute(last, axis, up)
        after = lax.ppermute(first, axis, down)
        value = jnp.concatenate([before, value, after], axis=dim)
    return value


def build_columns(fields, conduct, potential):
    center = fields[:, 1:-1, 1:-1]
    k_mid = conduct[1:-1, 1:-1]
    x_plus = 0.5 * (k_mid + conduct[2:, 1:-1])
    x_minus = 0.5 * (k_mid + conduct[:-2, 1:-1])
    y_plus = 0.5 * (k_mid + conduct[1:-1, 2:])
    y_minus = 0.5 * (k_mid + conduct[1:-1, :-2])
    along_x = x_plus * (center - fields[:, 2:, 1:-1]) + x_minus * (center - fields[:, :-2, 1:-1])
    along_y = y_plus * (center - fields[:, 1:-1, 2:]) + y_minus * (center - fields[:, 1:-1, :-2])
    react = potential * center
    stacked = jnp.concatenate([center, along_x, along_y, react], 0)
    return stacked.reshape(stacked.shape[0], -1)


def inner_products(matrix, cell_count):
    return jnp.dot(matrix, matrix.T, precision=lax.Precision.HIGHEST) / cell_count


def on_device(mode_fields, conductance, potential):
    modes_count = mode_fields.shape[0]
    rows_here = mode_fields.shape[1]
    cols_here = mode_fields.shape[2]
    stacked = jnp.concatenate([mode_fields, conductance[None]], 0)
    padded = padded_2(stacked, (("gx", 1), ("gy", 2)), 1)
    matrix = build_columns(padded[:modes_count], padded[modes_count], potential)
    cell_count = float(rows_here * cols_here * lax.axis_size("gx") * lax.axis_size("gy"))
    gram_total = lax.psum(inner_products(matrix, cell_count), ("gx", "gy"))
    lower_tri = jnp.linalg.cholesky(gram_total)
    basis_flat = jax.scipy.linalg.solve_triangular(lower_tri, matrix, lower=True)
    basis_field = basis_flat.reshape(basis_flat.shape[0], rows_here, cols_here)
    return (basis_field, lower_tri.T)


def solution(mesh):
    placed = (P(None, "gx", "gy"), P("gx", "gy"), P("gx", "gy"))
    return jax.shard_map(
        on_device, mesh=mesh, in_specs=placed, out_specs=(P(None, "gx", "gy"), P()), check_vma=False
    )
```

profile of v0, /device:TPU:1, one launch (start us, length us, event | category | flops | bytes accessed | tf_op | source)
XLA Modules:
  0.0 232.6 jit_solution(10538956578714779694)
XLA Ops:
  7.2 0.9 broadcast_in_dim.3
  8.1 5.0 %fusion.22 = (f32[32,64,256]{2,0,1:T(8,128)}, f32[33,64,256]{2,0,1:T(8,128)S(1)}, f32[32,64,256]{2,0,1:T(8,128)}) fusion(f32[32,64,256]{2,1,0:T(8,128)} %param.3, f32[64,256]{1,0:T(8,128)} %param.5), kind=kLoop, calls=%fused_computation.51 | loop fusion | flops 524287 | bytes 8454144 | tf_op args[0]
  13.1 0.9 dynamic-update-slice.4
  14.0 3.9 %collective-permute-start = (f32[33,1,256]{2,0,1:T(8,128)S(1)}, f32[33,1,256]{2,0,1:T(8,128)S(1)}, u32[]{:S(2)}, u32[]{:S(2)}) collective-permute-start(f32[33,1,256]{2,0,1:T(8,128)S(1)} %get-tuple-element.12), channel_id=1, source_target_pairs={{0,4},{4,8},{8,12},{12,16},{16,20},{20,24},{24,28},{1,5},{5,9},{9,... | collective-permute-start | bytes 101384 | tf_op jit(solution)/shard_map/ppermute | solution.py:14
  17.9 1.3 collective-permute-start.1
  19.2 3.4 %collective-permute-done.1 = f32[33,1,256]{2,0,1:T(8,128)S(1)} collective-permute-done((f32[33,1,256]{2,0,1:T(8,128)S(1)}, f32[33,1,256]{2,0,1:T(8,128)S(1)}, u32[]{:S(2)}, u32[]{:S(2)}) %collective-permute-start.1) | collective-permute-done | bytes 33824 | tf_op jit(solution)/shard_map/ppermute | solution.py:15
  22.8 1.9 fusion.20
  24.8 1.8 copy.32
  26.6 4.0 %collective-permute-start.3 = (f32[33,66,1]{1,2,0:T(1,128)S(1)}, f32[33,66,1]{1,2,0:T(1,128)S(1)}, u32[]{:S(2)}, u32[]{:S(2)}) collective-permute-start(f32[33,66,1]{1,2,0:T(1,128)S(1)} %copy.32), channel_id=1, source_target_pairs={{1,0},{2,1},{3,2},{5,4},{6,5},{7,6},{9,8},{10,9},{11,10},{13,12},{... | collective-permute-start | bytes 26144 | tf_op jit(solution)/shard_map/ppermute | solution.py:15
  30.6 1.8 copy.31
  32.4 3.1 %collective-permute-start.2 = (f32[33,66,1]{1,2,0:T(1,128)S(1)}, f32[33,66,1]{1,2,0:T(1,128)S(1)}, u32[]{:S(2)}, u32[]{:S(2)}) collective-permute-start(f32[33,66,1]{1,2,0:T(1,128)S(1)} %copy.31), channel_id=1, source_target_pairs={{0,1},{1,2},{2,3},{4,5},{5,6},{6,7},{8,9},{9,10},{10,11},{12,13},{... | collective-permute-start | bytes 26144 | tf_op jit(solution)/shard_map/ppermute | solution.py:14
  35.4 1.7 copy.34
  37.1 1.7 copy.33
  38.8 1.5 pad_maximum_fusion.10
  41.3 7.0 %fusion.9 = (f32[32,64,256]{2,0,1:T(8,128)}, f32[32,64,256]{2,0,1:T(8,128)}) fusion(f32[33,64,256]{2,0,1:T(8,128)S(1)} %dynamic-update-slice.4, f32[33,1,256]{2,0,1:T(8,128)S(1)} %collective-permute-done, f32[33,1,256]{2,0,1:T(8,128)S(1)} %collective-permute-done.1, f32[64,256]{1,0:T(8,128)S(1)} %get-tuple-element.19, f32[64,256]{1,0:T(8,128)S(1)} %get-tuple-element.17, ...), kind=kLoop, calls=%fused_computation.18 | loop fusion | flops 9437184 | bytes 8801296 | tf_op jit(solution)/shard_map/add | solution.py:27
  48.3 10.7 %fusion.12 = f32[128,128]{0,1:T(8,128)} fusion(f32[32,64,256]{2,0,1:T(8,128)} %get-tuple-element.16, f32[32,64,256]{2,0,1:T(8,128)} %get-tuple-element.9, f32[32,64,256]{2,0,1:T(8,128)} %get-tuple-element.8, f32[32,64,256]{2,0,1:T(8,128)S(1)} %copy-done.3), kind=kOutput, calls=%fused_computation.23 | convolution fusion | flops 3227533312 | bytes 8454144 | tf_op jit(solution)/shard_map/dot_general | solution.py:35
  59.0 5.7 %pad_maximum_fusion = f32[128,64,256]{2,0,1:T(8,128)} fusion(f32[32,64,256]{2,0,1:T(8,128)} %get-tuple-element.16, f32[32,64,256]{2,0,1:T(8,128)} %get-tuple-element.9, f32[32,64,256]{2,0,1:T(8,128)} %get-tuple-element.8, f32[32,64,256]{2,0,1:T(8,128)S(1)} %copy-done.4), kind=kLoop, calls=%fused_computation | loop fusion | flops 6291456 | bytes 16777216 | tf_op jit(solution)/shard_map/concatenate | solution.py:30
  64.7 9.0 %copy.45 = f32[128,64,256]{0,2,1:T(8,128)} copy(f32[128,64,256]{2,0,1:T(8,128)} %pad_maximum_fusion) | data formatting | bytes 16777216 | tf_op jit(solution)/shard_map/concatenate | solution.py:30
  73.7 107.6 %all-reduce.2.cloned.1.call-done = f32[128,128]{0,1:T(8,128)} async-done(((f32[128,128]{0,1:T(8,128)}), f32[128,128]{0,1:T(8,128)}) %all-reduce.2.cloned.1.call-update) | async-done | bytes 65552 | tf_op jit(solution)/shard_map/psum | solution.py:46
  181.3 0.9 copy.44
  183.1 11.7 %cholesky.16 = f32[128,128]{1,0:T(8,128)S(1)} custom-call(f32[128,128]{1,0:T(8,128)S(1)} %fusion.18), custom_call_target="Cholesky" | custom-call | tf_op jit(solution)/shard_map/jit(cholesky)/cholesky | solution.py:47
  196.9 9.8 %custom-call.7 = f32[1,128,128]{1,2,0:T(8,128)S(1)} custom-call(f32[1,128,128]{2,1,0:T(8,128)S(1)} %get-tuple-element.22), custom_call_target="InvertDiagBlocksLowerTriangular" | custom-call | tf_op jit(solution)/shard_map/jit(_solve_triangular)/triangular_solve | solution.py:48
  206.7 10.7 %fusion = f32[128,64,256]{2,0,1:T(8,128)S(1)} fusion(f32[128,64,256]{0,2,1:T(8,128)} %copy.45, f32[1,128,128]{1,2,0:T(8,128)S(1)} %custom-call.7), kind=kOutput, calls=%fused_computation.1 | convolution fusion | flops 3221225472 | bytes 16842752 | tf_op jit(solution)/shard_map/jit(_solve_triangular)/triangular_solve | solution.py:48
  217.5 8.3 %copy.47 = f32[128,64,256]{2,1,0:T(8,128)} copy(f32[128,64,256]{2,0,1:T(8,128)S(1)} %fusion) | data formatting | bytes 16777216
  (24 shorter events, 4.2 us)
Async XLA Ops:
  7.2 174.2 %all-reduce.2.cloned.1.call-start = ((), (), s32[]{:S(2)}) async-start(), calls=%async_computation | async-start | bytes 131072 | tf_op jit(solution)/shard_map/psum | solution.py:46
  14.0 5.2 %collective-permute-start = (f32[33,1,256]{2,0,1:T(8,128)S(1)}, f32[33,1,256]{2,0,1:T(8,128)S(1)}, u32[]{:S(2)}, u32[]{:S(2)}) collective-permute-start(f32[33,1,256]{2,0,1:T(8,128)S(1)} %get-tuple-element.12), channel_id=1, source_target_pairs={{0,4},{4,8},{8,12},{12,16},{16,20},{20,24},{24,28},{1,5},{5,9},{9,... | collective-permute-start | bytes 101384 | tf_op jit(solution)/shard_map/ppermute | solution.py:14
  17.9 4.7 %collective-permute-start.1 = (f32[33,1,256]{2,0,1:T(8,128)S(1)}, f32[33,1,256]{2,0,1:T(8,128)S(1)}, u32[]{:S(2)}, u32[]{:S(2)}) collective-permute-start(f32[33,1,256]{2,0,1:T(8,128)S(1)} %get-tuple-element.13), channel_id=1, source_target_pairs={{4,0},{8,4},{12,8},{16,12},{20,16},{24,20},{28,24},{5,1},{9,5},{13... | collective-permute-start | bytes 101384 | tf_op jit(solution)/shard_map/ppermute | solution.py:15
  26.6 8.9 %collective-permute-start.3 = (f32[33,66,1]{1,2,0:T(1,128)S(1)}, f32[33,66,1]{1,2,0:T(1,128)S(1)}, u32[]{:S(2)}, u32[]{:S(2)}) collective-permute-start(f32[33,66,1]{1,2,0:T(1,128)S(1)} %copy.32), channel_id=1, source_target_pairs={{1,0},{2,1},{3,2},{5,4},{6,5},{7,6},{9,8},{10,9},{11,10},{13,12},{... | collective-permute-start | bytes 26144 | tf_op jit(solution)/shard_map/ppermute | solution.py:15
  32.4 4.7 %collective-permute-start.2 = (f32[33,66,1]{1,2,0:T(1,128)S(1)}, f32[33,66,1]{1,2,0:T(1,128)S(1)}, u32[]{:S(2)}, u32[]{:S(2)}) collective-permute-start(f32[33,66,1]{1,2,0:T(1,128)S(1)} %copy.31), channel_id=1, source_target_pairs={{0,1},{1,2},{2,3},{4,5},{5,6},{6,7},{8,9},{9,10},{10,11},{12,13},{... | collective-permute-start | bytes 26144 | tf_op jit(solution)/shard_map/ppermute | solution.py:14
  38.8 1.7 copy-start
  38.8 1.9 copy-start.1
  38.8 2.6 %copy-start.2 = (f32[32,64,256]{2,1,0:T(8,128)S(1)}, f32[32,64,256]{2,1,0:T(8,128)}, u32[]{:S(2)}) copy-start(f32[32,64,256]{2,1,0:T(8,128)} %param.3) | copy-start | bytes 6291460
  41.3 7.0 %copy-start.3 = (f32[32,64,256]{2,0,1:T(8,128)S(1)}, f32[32,64,256]{2,0,1:T(8,128)}, u32[]{:S(2)}) copy-start(f32[32,64,256]{2,0,1:T(8,128)} %get-tuple-element.14) | copy-start | bytes 6291460
  48.3 10.7 %copy-start.4 = (f32[32,64,256]{2,0,1:T(8,128)S(1)}, f32[32,64,256]{2,0,1:T(8,128)}, u32[]{:S(2)}) copy-start(f32[32,64,256]{2,0,1:T(8,128)} %get-tuple-element.14) | copy-start | bytes 6291460
Sparse Core Ops, SparseCore 0:
  59.2 122.1 all-reduce.1
where the time goes:
time: 233 us
  waiting for transfers between devices  111 us (48%)
  other arithmetic  43.2 us (19%)
  local copies, waits for them, and re-layouts  30.4 us (13%)
  matrix products  21.4 us (9%)
  between operations  14.2 us (6%)
  starting transfers between devices  12.3 us (5%)
    psum x1, waiting for transfers between devices, on_device(): gram_total = lax.psum(inner_products(matrix, cell_count), ('gx', 'gy'))  108 us
    another operation x3, other arithmetic, on_device(): lower_tri = jnp.linalg.cholesky(gram_total)  12.4 us
    another operation x1, matrix products, on_device(): jax.scipy.linalg.solve_triangular(lower_tri, matrix, lower=True)  10.7 us
    dot_general x1, matrix products, inner_products(): jnp.dot(matrix, matrix.T, precision=lax.Precision.HIGHEST) / cell_count  10.7 us
    unnamed x13, local copies, waits for them, and re-layouts  9.88 us
    another operation x1, other arithmetic, on_device(): jax.scipy.linalg.solve_triangular(lower_tri, matrix, lower=True)  9.81 us
    concatenate x1, local copies, waits for them, and re-layouts, build_columns(): stacked = jnp.concatenate([center, along_x, along_y, react], 0)  9.01 us
    ppermute x2, starting transfers between devices, padded_2(): before = lax.ppermute(last, axis, up)  6.99 us
  transfers between devices with their start and end apart: 5, of which 2 were waited for; matrix products, arithmetic and copies ran while one was open for 8% of the time, Pallas kernels for 0%

commit v1 on v0

--- a/solution.py
+++ b/solution.py
@@ -43,7 +43,9 @@
     padded = padded_2(stacked, (("gx", 1), ("gy", 2)), 1)
     matrix = build_columns(padded[:modes_count], padded[modes_count], potential)
     cell_count = float(rows_here * cols_here * lax.axis_size("gx") * lax.axis_size("gy"))
-    gram_total = lax.psum(inner_products(matrix, cell_count), ("gx", "gy"))
+    gram_total = inner_products(matrix, cell_count)
+    for over in ("gy", "gx"):
+        gram_total = lax.psum(gram_total, over)
     lower_tri = jnp.linalg.cholesky(gram_total)
     basis_flat = jax.scipy.linalg.solve_triangular(lower_tri, matrix, lower=True)
     basis_field = basis_flat.reshape(basis_flat.shape[0], rows_here, cols_here)

time: 233 us -> 217 us (0.931); the launches traced: 233 us -> 214 us
  waiting for transfers between devices: 111 us -> 91.9 us
    psum x1 -> x2, waiting for transfers between devices: 108 us -> 88.4 us  [on_device(): gram_total = lax.psum(gram_total, over)]
  transfers between devices with their start and end apart: 5 -> 6, of which waited for: 2 -> 3; matrix products, arithmetic and copies ran while one was open for 8% -> 8% of each run, Pallas kernels for 0% -> 0%
where the time goes in v1:
time: 217 us; the launch traced here: 214 us
  waiting for transfers between devices  91.9 us (42%)
  other arithmetic  43.2 us (20%)
  local copies, waits for them, and re-layouts  30.4 us (14%)
  matrix products  21.4 us (10%)
  between operations  14.2 us (7%)
  starting transfers between devices  12.6 us (6%)
    psum x2, waiting for transfers between devices, on_device(): gram_total = lax.psum(gram_total, over)  88.4 us
    another operation x3, other arithmetic, on_device(): lower_tri = jnp.linalg.cholesky(gram_total)  12.4 us
    another operation x1, matrix products, on_device(): jax.scipy.linalg.solve_triangular(lower_tri, matrix, lower=True)  10.7 us
    dot_general x1, matrix products, inner_products(): jnp.dot(matrix, matrix.T, precision=lax.Precision.HIGHEST) / cell_count  10.7 us
    unnamed x13, local copies, waits for them, and re-layouts  9.88 us
    another operation x1, other arithmetic, on_device(): jax.scipy.linalg.solve_triangular(lower_tri, matrix, lower=True)  9.81 us
    concatenate x1, local copies, waits for them, and re-layouts, build_columns(): stacked = jnp.concatenate([center, along_x, along_y, react], 0)  9.01 us
    ppermute x2, starting transfers between devices, padded_2(): before = lax.ppermute(last, axis, up)  6.99 us
  transfers between devices with their start and end apart: 6, of which 3 were waited for; matrix products, arithmetic and copies ran while one was open for 8% of the time, Pallas kernels for 0%

profile of v1, /device:TPU:1, one launch (start us, length us, event | category | flops | bytes accessed | tf_op | source)
XLA Modules:
  0.0 213.7 jit_solution(12785266310437195147)
XLA Ops:
  7.2 0.9 broadcast_in_dim.3
  8.1 5.0 %fusion.22 = (f32[32,64,256]{2,0,1:T(8,128)}, f32[33,64,256]{2,0,1:T(8,128)S(1)}, f32[32,64,256]{2,0,1:T(8,128)}) fusion(f32[32,64,256]{2,1,0:T(8,128)} %param.3, f32[64,256]{1,0:T(8,128)} %param.5), kind=kLoop, calls=%fused_computation.51 | loop fusion | flops 524287 | bytes 8454144 | tf_op args[0]
  14.0 3.9 %collective-permute-start = (f32[33,1,256]{2,0,1:T(8,128)S(1)}, f32[33,1,256]{2,0,1:T(8,128)S(1)}, u32[]{:S(2)}, u32[]{:S(2)}) collective-permute-start(f32[33,1,256]{2,0,1:T(8,128)S(1)} %get-tuple-element.12), channel_id=1, source_target_pairs={{0,4},{4,8},{8,12},{12,16},{16,20},{20,24},{24,28},{1,5},{5,9},{9,... | collective-permute-start | bytes 101384 | tf_op jit(solution)/shard_map/ppermute | solution.py:14
  17.9 1.3 collective-permute-start.1
  19.2 3.4 %collective-permute-done.1 = f32[33,1,256]{2,0,1:T(8,128)S(1)} collective-permute-done((f32[33,1,256]{2,0,1:T(8,128)S(1)}, f32[33,1,256]{2,0,1:T(8,128)S(1)}, u32[]{:S(2)}, u32[]{:S(2)}) %collective-permute-start.1) | collective-permute-done | bytes 33824 | tf_op jit(solution)/shard_map/ppermute | solution.py:15
  22.8 1.9 fusion.20
  24.8 1.8 copy.32
  26.6 4.0 %collective-permute-start.3 = (f32[33,66,1]{1,2,0:T(1,128)S(1)}, f32[33,66,1]{1,2,0:T(1,128)S(1)}, u32[]{:S(2)}, u32[]{:S(2)}) collective-permute-start(f32[33,66,1]{1,2,0:T(1,128)S(1)} %copy.32), channel_id=1, source_target_pairs={{1,0},{2,1},{3,2},{5,4},{6,5},{7,6},{9,8},{10,9},{11,10},{13,12},{... | collective-permute-start | bytes 26144 | tf_op jit(solution)/shard_map/ppermute | solution.py:15
  30.6 1.8 copy.31
  32.4 3.1 %collective-permute-start.2 = (f32[33,66,1]{1,2,0:T(1,128)S(1)}, f32[33,66,1]{1,2,0:T(1,128)S(1)}, u32[]{:S(2)}, u32[]{:S(2)}) collective-permute-start(f32[33,66,1]{1,2,0:T(1,128)S(1)} %copy.31), channel_id=1, source_target_pairs={{0,1},{1,2},{2,3},{4,5},{5,6},{6,7},{8,9},{9,10},{10,11},{12,13},{... | collective-permute-start | bytes 26144 | tf_op jit(solution)/shard_map/ppermute | solution.py:14
  35.4 1.7 copy.34
  37.1 1.7 copy.33
  38.8 1.5 pad_maximum_fusion.10
  41.3 7.0 %fusion.9 = (f32[32,64,256]{2,0,1:T(8,128)}, f32[32,64,256]{2,0,1:T(8,128)}) fusion(f32[33,64,256]{2,0,1:T(8,128)S(1)} %dynamic-update-slice.4, f32[33,1,256]{2,0,1:T(8,128)S(1)} %collective-permute-done, f32[33,1,256]{2,0,1:T(8,128)S(1)} %collective-permute-done.1, f32[64,256]{1,0:T(8,128)S(1)} %get-tuple-element.19, f32[64,256]{1,0:T(8,128)S(1)} %get-tuple-element.17, ...), kind=kLoop, calls=%fused_computation.18 | loop fusion | flops 9437184 | bytes 8801296 | tf_op jit(solution)/shard_map/add | solution.py:27
  48.3 10.7 %fusion.12 = f32[128,128]{0,1:T(8,128)} fusion(f32[32,64,256]{2,0,1:T(8,128)} %get-tuple-element.16, f32[32,64,256]{2,0,1:T(8,128)} %get-tuple-element.9, f32[32,64,256]{2,0,1:T(8,128)} %get-tuple-element.8, f32[32,64,256]{2,0,1:T(8,128)S(1)} %copy-done.3), kind=kOutput, calls=%fused_computation.23 | convolution fusion | flops 3227533312 | bytes 8454144 | tf_op jit(solution)/shard_map/dot_general | solution.py:35
  59.3 30.9 %all-reduce.3.cloned.1.call-done = f32[128,128]{0,1:T(8,128)} async-done(((f32[128,128]{0,1:T(8,128)}), f32[128,128]{0,1:T(8,128)}) %all-reduce.3.cloned.1.call-update) | async-done | bytes 65552 | tf_op jit(solution)/shard_map/psum | solution.py:48
  90.2 5.7 %pad_maximum_fusion = f32[128,64,256]{2,0,1:T(8,128)} fusion(f32[32,64,256]{2,0,1:T(8,128)} %get-tuple-element.16, f32[32,64,256]{2,0,1:T(8,128)} %get-tuple-element.9, f32[32,64,256]{2,0,1:T(8,128)} %get-tuple-element.8, f32[32,64,256]{2,0,1:T(8,128)S(1)} %copy-done.4), kind=kLoop, calls=%fused_computation | loop fusion | flops 6291456 | bytes 16777216 | tf_op jit(solution)/shard_map/concatenate | solution.py:30
  95.9 9.0 %copy.45 = f32[128,64,256]{0,2,1:T(8,128)} copy(f32[128,64,256]{2,0,1:T(8,128)} %pad_maximum_fusion) | data formatting | bytes 16777216 | tf_op jit(solution)/shard_map/concatenate | solution.py:30
  104.9 57.6 %all-reduce.5.cloned.1.call-done = f32[128,128]{0,1:T(8,128)} async-done(((f32[128,128]{0,1:T(8,128)}), f32[128,128]{0,1:T(8,128)}) %all-reduce.5.cloned.1.call-update) | async-done | bytes 65552 | tf_op jit(solution)/shard_map/psum | solution.py:48
  162.4 0.9 copy.44
  164.2 11.7 %cholesky.16 = f32[128,128]{1,0:T(8,128)S(1)} custom-call(f32[128,128]{1,0:T(8,128)S(1)} %fusion.18), custom_call_target="Cholesky" | custom-call | tf_op jit(solution)/shard_map/jit(cholesky)/cholesky | solution.py:49
  178.0 9.8 %custom-call.7 = f32[1,128,128]{1,2,0:T(8,128)S(1)} custom-call(f32[1,128,128]{2,1,0:T(8,128)S(1)} %get-tuple-element.22), custom_call_target="InvertDiagBlocksLowerTriangular" | custom-call | tf_op jit(solution)/shard_map/jit(_solve_triangular)/triangular_solve | solution.py:50
  187.8 10.7 %fusion = f32[128,64,256]{2,0,1:T(8,128)S(1)} fusion(f32[128,64,256]{0,2,1:T(8,128)} %copy.45, f32[1,128,128]{1,2,0:T(8,128)S(1)} %custom-call.7), kind=kOutput, calls=%fused_computation.1 | convolution fusion | flops 3221225472 | bytes 16842752 | tf_op jit(solution)/shard_map/jit(_solve_triangular)/triangular_solve | solution.py:50
  198.6 8.3 %copy.47 = f32[128,64,256]{2,1,0:T(8,128)} copy(f32[128,64,256]{2,0,1:T(8,128)S(1)} %fusion) | data formatting | bytes 16777216
  (27 shorter events, 5.3 us)
Async XLA Ops:
  7.2 83.0 %all-reduce.3.cloned.1.call-start = ((), (), s32[]{:S(2)}) async-start(), calls=%async_computation | async-start | bytes 131072 | tf_op jit(solution)/shard_map/psum | solution.py:48
  14.0 5.2 %collective-permute-start = (f32[33,1,256]{2,0,1:T(8,128)S(1)}, f32[33,1,256]{2,0,1:T(8,128)S(1)}, u32[]{:S(2)}, u32[]{:S(2)}) collective-permute-start(f32[33,1,256]{2,0,1:T(8,128)S(1)} %get-tuple-element.12), channel_id=1, source_target_pairs={{0,4},{4,8},{8,12},{12,16},{16,20},{20,24},{24,28},{1,5},{5,9},{9,... | collective-permute-start | bytes 101384 | tf_op jit(solution)/shard_map/ppermute | solution.py:14
  17.9 4.7 %collective-permute-start.1 = (f32[33,1,256]{2,0,1:T(8,128)S(1)}, f32[33,1,256]{2,0,1:T(8,128)S(1)}, u32[]{:S(2)}, u32[]{:S(2)}) collective-permute-start(f32[33,1,256]{2,0,1:T(8,128)S(1)} %get-tuple-element.13), channel_id=1, source_target_pairs={{4,0},{8,4},{12,8},{16,12},{20,16},{24,20},{28,24},{5,1},{9,5},{13... | collective-permute-start | bytes 101384 | tf_op jit(solution)/shard_map/ppermute | solution.py:15
  26.6 8.9 %collective-permute-start.3 = (f32[33,66,1]{1,2,0:T(1,128)S(1)}, f32[33,66,1]{1,2,0:T(1,128)S(1)}, u32[]{:S(2)}, u32[]{:S(2)}) collective-permute-start(f32[33,66,1]{1,2,0:T(1,128)S(1)} %copy.32), channel_id=1, source_target_pairs={{1,0},{2,1},{3,2},{5,4},{6,5},{7,6},{9,8},{10,9},{11,10},{13,12},{... | collective-permute-start | bytes 26144 | tf_op jit(solution)/shard_map/ppermute | solution.py:15
  32.4 4.7 %collective-permute-start.2 = (f32[33,66,1]{1,2,0:T(1,128)S(1)}, f32[33,66,1]{1,2,0:T(1,128)S(1)}, u32[]{:S(2)}, u32[]{:S(2)}) collective-permute-start(f32[33,66,1]{1,2,0:T(1,128)S(1)} %copy.31), channel_id=1, source_target_pairs={{0,1},{1,2},{2,3},{4,5},{5,6},{6,7},{8,9},{9,10},{10,11},{12,13},{... | collective-permute-start | bytes 26144 | tf_op jit(solution)/shard_map/ppermute | solution.py:14
  38.8 1.7 copy-start
  38.8 1.9 copy-start.1
  38.8 2.6 %copy-start.2 = (f32[32,64,256]{2,1,0:T(8,128)S(1)}, f32[32,64,256]{2,1,0:T(8,128)}, u32[]{:S(2)}) copy-start(f32[32,64,256]{2,1,0:T(8,128)} %param.3) | copy-start | bytes 6291460
  41.3 7.0 %copy-start.3 = (f32[32,64,256]{2,0,1:T(8,128)S(1)}, f32[32,64,256]{2,0,1:T(8,128)}, u32[]{:S(2)}) copy-start(f32[32,64,256]{2,0,1:T(8,128)} %get-tuple-element.14) | copy-start | bytes 6291460
  48.3 41.8 %copy-start.4 = (f32[32,64,256]{2,0,1:T(8,128)S(1)}, f32[32,64,256]{2,0,1:T(8,128)}, u32[]{:S(2)}) copy-start(f32[32,64,256]{2,0,1:T(8,128)} %get-tuple-element.14) | copy-start | bytes 6291460
  59.0 103.4 %all-reduce.5.cloned.1.call-start = ((), (), s32[]{:S(2)}) async-start(), calls=%async_computation.1 | async-start | bytes 131072 | tf_op jit(solution)/shard_map/psum | solution.py:48
Sparse Core Ops, SparseCore 0:
  59.2 30.9 all-reduce.2
  93.5 68.8 all-reduce.4
